TPU v7x, 32 devices: a whole 2x2x4 slice. The times are simulated.
32 devices in a mesh: rows: 8 (over z, y), grp: 4 (over x, core).
Axes of the slice: x: 2, y: 2, z: 4, core: 2. Of those that a mesh axis runs over, the one named last changes fastest.
Arguments:
- features: float32 [8192, 128], P(('rows', 'grp'))
- key_ids: int32 [8192], P(('rows', 'grp')), may hold values from 0 to 23, as said below
- owner: int32 [24], replicated, may hold values from 0 to 23, each once
Outputs:
- covariance: float32 [3072, 128], P(('rows', 'grp'))
Inputs may be any that keep to these rules, and one draw needn't show every extreme that they name: `key_ids`: every key is the key of at least 2 rows.
All inputs are finite; a program needn't handle non-finite values.
Results may differ from a plain program's by a relative error of at most 0.0003.
Values sent between devices are 32-bit elements; how exact they have to be, the bound alone decides.
A program may use at most 64 MiB of HBM per device.

v0:
```python
import jax
import jax.numpy as jnp
from jax import lax
from jax.sharding import PartitionSpec as P


def local(features, key_ids, owner):
    nkeys = owner.shape[0]
    width = features.shape[1]
    labels = jnp.arange(nkeys, dtype=jnp.int32)
    member = key_ids[:, None] == labels[None, :]
    slot = jnp.sum(jnp.where(member, owner[None, :], 0), axis=1)
    onehot = (slot[:, None] == labels[None, :]).astype(jnp.float32)
    contract = (((0,), (0,)), ((), ()))
    local_total = lax.dot_general(
        onehot,
        features,
        contract,
        precision=lax.Precision.HIGHEST,
        preferred_element_type=jnp.float32,
    )
    local_count = jnp.sum(onehot, axis=0)
    weighted = (onehot[:, :, None] * features[:, None, :]).reshape(features.shape[0], nkeys * width)
    gram_flat = lax.dot_general(
        weighted,
        features,
        contract,
        precision=lax.Precision.HIGHEST,
        preferred_element_type=jnp.float32,
    )
    n_rows = lax.axis_size("rows")
    n_grp = lax.axis_size("grp")
    local_rows = nkeys * width // (n_rows * n_grp)
    partial_value = lax.psum_scatter(gram_flat, "rows", scatter_dimension=0, tiled=True)
    received = lax.psum_scatter(partial_value, "grp", scatter_dimension=0, tiled=True)
    position = lax.axis_index("rows") * n_grp + lax.axis_index("grp")
    base = position * local_rows
    target = base + jnp.arange(local_rows, dtype=jnp.int32)
    owner_slot = target // width
    column = target % width
    total, count = lax.psum((local_total, local_count), ("rows", "grp"))
    slot_total = jnp.take(total, owner_slot, axis=0)
    slot_count = jnp.take(count, owner_slot, axis=0)[:, None]
    own_total = jnp.take_along_axis(slot_total, column[:, None], axis=1)
    centred = received - own_total * slot_total / slot_count
    return centred / (slot_count - 1.0)


def solution(mesh):
    placed = (P(("rows", "grp"), None), P(("rows", "grp")), P())
    return jax.shard_map(
        local, mesh=mesh, in_specs=placed, out_specs=P(("rows", "grp"), None), check_vma=False
    )
```

profile of v0, /device:TPU:0, one launch (start us, length us, event | category | flops | bytes accessed | tf_op | source)
XLA Modules:
  0.0 113.6 jit_solution(11234650140521624888)
XLA Ops:
  6.5 0.0 copy-start
  6.5 0.0 reduce-scatter.3.cloned.1.call-start
  6.5 0.8 select_reduce_fusion
  7.4 0.1 copy.4
  7.5 1.8 %broadcast_multiply_fusion = f32[256,24,128]{2,1,0:T(8,128)S(1)} fusion(f32[256,128]{1,0:T(8,128)} %param.3, f32[256,24]{1,0:T(8,128)S(1)} %copy.4), kind=kLoop, calls=%fused_computation.6 | loop fusion | flops 786432 | bytes 3301376 | tf_op jit(solution)/shard_map/mul | solution.py:23
  9.3 0.0 copy-done
  9.3 6.2 %fusion = f32[3072,128]{1,0:T(8,128)} fusion(f32[256,128]{1,0:T(8,128)S(1)} %copy-done, f32[32,8,24,128]{3,2,1,0:T(8,128)S(1)} %bitcast.12), kind=kOutput, calls=%fused_computation.3 | convolution fusion | flops 1207959552 | bytes 4849664 | tf_op jit(solution)/shard_map/dot_general | solution.py:24
  15.5 0.0 reduce-scatter.3.cloned.1.call-update
  15.5 0.0 reduce-scatter.5.cloned.1.call-start
  15.6 0.1 fusion.6
  15.7 0.2 fusion.3
  15.8 42.8 %all-reduce = (f32[24,128]{1,0:T(8,128)S(1)}, f32[24]{0:T(128)S(1)}) all-reduce(f32[24,128]{1,0:T(8,128)S(1)} %fusion.3, f32[24]{0:T(128)S(1)} %fusion.6), channel_id=1, replica_groups=mesh['rows'=8,'grp'=4] {'rows','grp'}, use_global_device_ids=true, to_apply=%region_3.4 | all-reduce | flops 3096 | bytes 24768 | tf_op jit(solution)/shard_map/psum | solution.py:41
  58.6 1.2 %gather_fusion.1 = f32[96]{0:T(128)S(1)} fusion(f32[24]{0:T(128)S(1)} %get-tuple-element.6, s32[1024]{0:T(1024)S(1)} %pad_clamp_fusion), kind=kCustom, calls=%fused_computation.1 | custom fusion | bytes 1152 | tf_op jit(solution)/shard_map/jit(_take)/gather | solution.py:43
  59.9 0.6 gather_fusion
  60.6 0.1 broadcast_select_fusion
  60.6 23.5 %reduce-scatter.3.cloned.1.call-done = f32[384,128]{1,0:T(8,128)} async-done(((f32[3072,128]{1,0:T(8,128)}), f32[384,128]{1,0:T(8,128)}) %reduce-scatter.3.cloned.1.call-update) | async-done | bytes 196624 | tf_op jit(solution)/shard_map/reduce_scatter | solution.py:34
  84.1 0.0 reduce-scatter.5.cloned.1.call-update
  84.2 1.2 %gather_fusion.2 = f32[96]{0:T(128)S(1)} fusion(f32[96,128]{1,0:T(8,128)S(1)} %broadcast_select_fusion, s32[96]{0:T(128)S(1)} %or_bitcast_fusion), kind=kCustom, calls=%fused_computation.2 | custom fusion | bytes 1536 | tf_op jit(solution)/shard_map/jit(take_along_axis)/gather | solution.py:44
  85.4 19.8 %reduce-scatter.5.cloned.1.call-done = f32[96,128]{1,0:T(8,128)} async-done(((f32[384,128]{1,0:T(8,128)}), f32[96,128]{1,0:T(8,128)}) %reduce-scatter.5.cloned.1.call-update) | async-done | bytes 49168 | tf_op jit(solution)/shard_map/reduce_scatter | solution.py:35
  105.2 1.5 %subtract_divide_fusion = f32[96,128]{1,0:T(8,128)} fusion(f32[96,128]{1,0:T(8,128)} %reduce-scatter.5.cloned.1.call-done, f32[96]{0:T(128)S(1)} %get-tuple-element.7, f32[96]{0:T(128)S(1)} %get-tuple-element.8, f32[96]{0:T(128)S(1)} %get-tuple-element.9, f32[96,128]{1,0:T(8,128)S(1)} %gather_fusion, pred[96]{0:T(512)(128)(4,1)S(1)} %compare_and_fusion), kind=kLoop, calls=%fused_computation.7 | loop fusion | flops 61440 | bytes 148704 | tf_op jit(solution)/shard_map/div | solution.py:46
  (9 shorter events, 0.1 us)
Async XLA Ops:
  6.5 2.7 %copy-start = (f32[256,128]{1,0:T(8,128)S(1)}, f32[256,128]{1,0:T(8,128)}, u32[]{:S(2)}) copy-start(f32[256,128]{1,0:T(8,128)} %param.3) | copy-start | bytes 393220
  6.5 77.6 %reduce-scatter.3.cloned.1.call-start = ((), (), s32[]{:S(2)}) async-start(), calls=%async_computation.2 | async-start | bytes 1769472 | tf_op jit(solution)/shard_map/reduce_scatter | solution.py:34
  15.5 89.7 %reduce-scatter.5.cloned.1.call-start = ((), (), s32[]{:S(2)}) async-start(), calls=%async_computation.3 | async-start | bytes 245760 | tf_op jit(solution)/shard_map/reduce_scatter | solution.py:35
Sparse Core Ops, SparseCore 0:
  15.6 68.4 reduce-scatter.2
  86.6 18.5 reduce-scatter.4
where the time goes:
time: 114 us
  waiting for transfers between devices  43.3 us (38%)
  blocking collectives  42.8 us (38%)
  between operations  13.5 us (12%)
  matrix products  6.39 us (6%)
  other arithmetic  4.42 us (4%)
  local copies, waits for them, and re-layouts  3.2 us (3%)
    psum x1, blocking collectives, local(): total, count = lax.psum((local_total, local_count), ('rows', 'grp'))  42.8 us
    reduce_scatter x1, waiting for transfers between devices, local(): lax.psum_scatter(gram_flat, 'rows', scatter_dimension=0, tiled=True)  23.5 us
    reduce_scatter x1, waiting for transfers between devices, local(): lax.psum_scatter(partial_value, 'grp', scatter_dimension=0, tiled=True)  19.8 us
    dot_general x1, matrix products, local(): lax.dot_general(weighted, features, contract, precision=lax.Precision.HIG...  6.23 us
  transfers between devices with their start and end apart: 2, of which 2 were waited for; matrix products, arithmetic and copies ran while one was open for 3% of the time, Pallas kernels for 0%

commit v1 on v0

v1 whole, which is shorter than its diff:
```python
import functools

import jax
import jax.numpy as jnp
from jax import lax
from jax.experimental import pallas as pl
from jax.experimental.pallas import tpu as pltpu
from jax.sharding import PartitionSpec as P

MESH = pl.DeviceIdType.MESH
LANES = 128
TAIL = 8


def flip(q, mask):
    bit = 1
    while bit <= mask:
        if mask & bit:
            q = q + bit * (1 - 2 * ((q // bit) % 2))
        bit *= 2
    return q


def kernel(
    inner, n_grp, n_line, nkeys, length, padded,
    feat_ref, key_ref, owner_ref, out_ref,
    blocks, keys, part, arrived, load_sem, send_sem, recv_sem, line_send, line_recv,
):
    group = inner * n_grp
    nrows, width = feat_ref.shape
    r, g = lax.axis_index("rows"), lax.axis_index("grp")
    line = r // inner
    q = (r % inner) * n_grp + g

    def peer(mask):
        other = flip(q, mask)
        return (line * inner + other // n_grp, other % n_grp)

    def along(step):
        return (((line + step) % n_line) * inner + r % inner, g)

    loads = [
        pltpu.make_async_copy(feat_ref, blocks.at[0], load_sem.at[0]),
        pltpu.make_async_copy(key_ref, keys.at[0], load_sem.at[1]),
    ]
    for copy in loads:
        copy.start()
    far = list(range(2, group, 2))
    barrier = pltpu.get_barrier_semaphore()
    for mask in [1] + far:
        pl.semaphore_signal(barrier, inc=1, device_id=peer(mask), device_id_type=MESH)
    if n_line <= 8:
        for step in range(1, n_line):
            pl.semaphore_signal(barrier, inc=1, device_id=along(step), device_id_type=MESH)
    else:
        def greet(step, c):
            pl.semaphore_signal(barrier, inc=1, device_id=along(step), device_id_type=MESH)
            return c
        lax.fori_loop(1, n_line, greet, 0)

    lane = lax.broadcasted_iota(jnp.int32, (1, LANES), 1)
    inverse = jnp.zeros((1, LANES), jnp.int32)
    for k in range(nkeys):
        inverse = jnp.where(lane == owner_ref[k], k + 1, inverse)
    row = lax.broadcasted_iota(jnp.int32, (padded + TAIL, 1), 0)

    def base_of(step):
        return (((line + step) % n_line) * group + q) * length

    def wanted(step):
        base = base_of(step)
        tail = (row - padded) % (TAIL // 2)
        slot = jnp.where(row < padded, (base + row) // width, base // width + tail)
        last = (base + length - 1) // width
        none = ((row >= length) & (row < padded)) | (slot > last)
        slot = jnp.where(none, -1, slot)
        found = jnp.where(lane == slot, inverse, 0)
        return jnp.sum(found, axis=1, keepdims=True) - 1

    shared = (group * length) % width == 0
    unroll = n_line <= 8
    wants = [wanted(step) for step in range(n_line)] if unroll else None

    def values(block, step):
        offset = base_of(step) % width
        turned = pltpu.roll(block, (width - offset) % width, 1)
        return jnp.transpose(turned)[:padded]

    def piece(slot, step, first, block, key_row, flat):
        want = wants[step] if unroll else wanted(step)
        if flat is None:
            flat = values(block, step)
        flat = jnp.concatenate([flat, jnp.ones((TAIL, nrows), jnp.float32)], axis=0)
        picked = jnp.where(key_row == want, flat, 0.0)
        gram = jnp.dot(
            picked, block, precision=lax.Precision.HIGHEST, preferred_element_type=jnp.float32
        )
        count = jnp.sum(picked[padded:], axis=1, keepdims=True)
        tail_row = lax.broadcasted_iota(jnp.int32, (TAIL, width), 0)
        tail = jnp.where(tail_row < TAIL // 2, gram[padded:], count)
        if first:
            part[step, :padded] = gram[:padded]
            part[step, padded:] = tail
        else:
            part[step, :padded] += gram[:padded]
            part[step, padded:] += tail

    def line_copy(step):
        return pltpu.make_async_remote_copy(
            src_ref=part.at[step], dst_ref=arrived.at[step],
            send_sem=line_send.at[step], recv_sem=line_recv.at[step],
            device_id=along(step), device_id_type=MESH,
        )

    def compute(slot, first=False, final=False):
        block = blocks[slot]
        key_row = jnp.concatenate(
            [keys[slot, i : i + 1, :] for i in range(nrows // LANES)], axis=1
        )
        flat = values(block, 0) if shared else None
        if unroll:
            for step in list(range(1, n_line)) + [0]:
                piece(slot, step, first, block, key_row, flat)
                if final and step:
                    line_copy(step).start()
        else:
            def body(step, c):
                piece(slot, step, first, block, key_row, flat)
                return c
            lax.fori_loop(0, n_line, body, 0)
            if final:
                def send(step, c):
                    line_copy(step).start()
                    return c
                lax.fori_loop(1, n_line, send, 0)

    def copies(src, dst, device, index):
        return [
            pltpu.make_async_remote_copy(
                src_ref=buf.at[src], dst_ref=buf.at[dst],
                send_sem=send_sem.at[i, index], recv_sem=recv_sem.at[i, dst],
                device_id=device, device_id_type=MESH,
            )
            for i, buf in enumerate((keys, blocks))
        ]

    for copy in loads:
        copy.wait()
    n_meet = len(far) + n_line
    pl.semaphore_wait(barrier, n_meet)

    sent = []

    def send(src, dst, device):
        for copy in copies(src, dst, device, len(sent)):
            copy.start()
        sent.append((src, dst, device, len(sent)))

    def receive(slot):
        for copy in copies(slot, slot, peer(1), 0):
            copy.wait_recv()

    for mask in far:
        send(0, mask, peer(mask))
    send(0, 1, peer(1))
    compute(0, first=True)
    receive(1)
    compute(1)
    near = far[:-1]
    for mask in near:
        receive(mask)
        send(mask, mask ^ 1, peer(1))
    for mask in near:
        compute(mask)
    for mask in near:
        receive(mask ^ 1)
        compute(mask ^ 1)
    for mask in far[-1:]:
        receive(mask)
        send(mask, mask ^ 1, peer(1))
        compute(mask)
        receive(mask ^ 1)
        compute(mask ^ 1, final=True)

    def collect(step, total):
        line_copy(step).wait_recv()
        return total + arrived[step]

    total = part[0]
    if unroll:
        for step in range(1, n_line):
            total = collect(step, total)
    else:
        total = lax.fori_loop(1, n_line, collect, total)

    base = base_of(0)
    index = lax.broadcasted_iota(jnp.int32, (padded, width), 0)
    column = lax.broadcasted_iota(jnp.int32, (padded, width), 1)
    flat_row = base + index
    segment = flat_row // width - base // width
    half = TAIL // 2
    sums = total[padded : padded + 1]
    count = total[padded + half : padded + half + 1]
    sums = jnp.broadcast_to(sums, (padded, width))
    count = jnp.broadcast_to(count, (padded, width))
    for s in range(1, half):
        sums = jnp.where(segment == s, total[padded + s : padded + s + 1], sums)
        count = jnp.where(segment == s, total[padded + half + s : padded + half + s + 1], count)
    own = jnp.sum(jnp.where(column == flat_row % width, sums, 0.0), axis=1, keepdims=True)
    result = (total[:padded] - own * sums / count) / (count - 1.0)
    out_ref[...] = result[:length]

    for item in sent:
        for copy in copies(*item):
            copy.wait_send()
    if unroll:
        for step in range(1, n_line):
            line_copy(step).wait_send()
    else:
        def drain(step, c):
            line_copy(step).wait_send()
            return c
        lax.fori_loop(1, n_line, drain, 0)


def solution(mesh):
    n_rows, n_grp = mesh.shape["rows"], mesh.shape["grp"]
    inner = 2
    group = inner * n_grp

    def local(features, key_ids, owner):
        nkeys = owner.shape[0]
        rows, width = features.shape
        length = nkeys * width // (n_rows * n_grp)
        padded = -(-length // 8) * 8
        n_line = n_rows // inner
        assert padded <= width == LANES and nkeys <= LANES and group & (group - 1) == 0
        keys = key_ids.reshape(rows // LANES, LANES)
        n_sent = group
        return pl.pallas_call(
            functools.partial(kernel, inner, n_grp, n_line, nkeys, length, padded),
            out_shape=jax.ShapeDtypeStruct((length, width), jnp.float32),
            in_specs=[
                pl.BlockSpec(memory_space=pltpu.MemorySpace.HBM),
                pl.BlockSpec(memory_space=pltpu.MemorySpace.HBM),
                pl.BlockSpec(memory_space=pltpu.MemorySpace.SMEM),
            ],
            out_specs=pl.BlockSpec(memory_space=pltpu.MemorySpace.VMEM),
            scratch_shapes=[
                pltpu.VMEM((group, rows, width), jnp.float32),
                pltpu.VMEM((group, rows // LANES, LANES), jnp.int32),
                pltpu.VMEM((n_line, padded + TAIL, width), jnp.float32),
                pltpu.VMEM((n_line, padded + TAIL, width), jnp.float32),
                pltpu.SemaphoreType.DMA((2,)),
                pltpu.SemaphoreType.DMA((2, n_sent)),
                pltpu.SemaphoreType.DMA((2, group)),
                pltpu.SemaphoreType.DMA((n_line,)),
                pltpu.SemaphoreType.DMA((n_line,)),
            ],
            compiler_params=pltpu.CompilerParams(collective_id=0, has_side_effects=True),
        )(features, keys, owner)

    placed = (P(("rows", "grp"), None), P(("rows", "grp")), P())
    return jax.shard_map(
        local, mesh=mesh, in_specs=placed, out_specs=P(("rows", "grp"), None), check_vma=False
    )
```

time: 114 us -> 23.9 us (0.21)
  waiting for transfers between devices: 43.3 us -> 0 us
  blocking collectives: 42.8 us -> 0 us
  Pallas kernels: 0 us -> 22.2 us
  between operations: 13.5 us -> 0.01 us
  matrix products: 6.39 us -> 0 us
  other arithmetic: 4.42 us -> 0 us
  local copies, waits for them, and re-layouts: 3.2 us -> 1.42 us
    reduce_scatter x2 -> x0, waiting for transfers between devices: 43.2 us -> none  [the longest x1 23.5 us: local(): lax.psum_scatter(gram_flat, 'rows', scatter_dimension=0, tiled=True)]
    psum x1 -> x0, blocking collectives: 42.8 us -> none  [local(): total, count = lax.psum((local_total, local_count), ('rows', 'grp'))]
    pallas_call x0 -> x1, Pallas kernels: none -> 22.2 us  [local(): pl.pallas_call(functools.partial(kernel, inner, n_grp, n_line, nkeys, len...]
    dot_general x2 -> x0, matrix products: 6.39 us -> none  [the longest x1 6.23 us: local(): lax.dot_general(weighted, features, contract, precision=lax.Precision.HIG...]
    gather x3 -> x0, local copies, waits for them, and re-layouts: 3.09 us -> none  [the longest x1 1.25 us: local(): own_total = jnp.take_along_axis(slot_total, column[:, None], axis=1)]
    mul x1 -> x0, other arithmetic: 1.78 us -> none  [local(): onehot[:, :, None] * features[:, None, :]]
    div x1 -> x0, other arithmetic: 1.54 us -> none  [local(): return centred / (slot_count - 1.0)]
    unnamed x3 -> x1, local copies, waits for them, and re-layouts: 0.01 us -> 1.42 us
  transfers between devices with their start and end apart: 2 -> 0, of which waited for: 2 -> 0; matrix products, arithmetic and copies ran while one was open for 3% -> 0% of each run, Pallas kernels for 0% -> 0%
where the time goes in v1:
time: 23.9 us; the launch traced here: 23.7 us
  Pallas kernels  22.2 us (93%)
  local copies, waits for them, and re-layouts  1.42 us (6%)
    pallas_call x1, Pallas kernels, local(): pl.pallas_call(functools.partial(kernel, inner, n_grp, n_line, nkeys, len...  22.2 us
    unnamed x1, local copies, waits for them, and re-layouts  1.42 us

profile of v1, /device:TPU:0, one launch (start us, length us, event | category | flops | bytes accessed | tf_op | source)
XLA Modules:
  0.0 23.7 jit_solution(6071927495915418224)
XLA Ops:
  0.0 22.2 %shard_map.37 = f32[96,128]{1,0:T(8,128)} custom-call(f32[256,128]{1,0:T(8,128)} %feat_ref.1, s32[2,128]{1,0:T(2,128)} %bitcast.1, s32[24]{0:T(128)} %owner_ref.1), custom_call_target="tpu_custom_call" | custom-call | tf_op jit(solution)/shard_map/pallas_call | solution.py:240
  22.3 1.4 %copy.5 = f32[96,128]{1,0:T(8,128)} copy(f32[96,128]{1,0:T(8,128)} %shard_map.37) | data formatting | bytes 98304

commit v2 on v1

--- a/solution.py
+++ b/solution.py
@@ -24,7 +24,8 @@
 def kernel(
     inner, n_grp, n_line, nkeys, length, padded,
     feat_ref, key_ref, owner_ref, out_ref,
-    blocks, keys, part, arrived, load_sem, send_sem, recv_sem, line_send, line_recv,
+    owner_smem, blocks, keys, part, arrived, load_sem, send_sem, recv_sem, key_send, key_recv,
+    line_send, line_recv,
 ):
     group = inner * n_grp
     nrows, width = feat_ref.shape
@@ -42,12 +43,12 @@
     loads = [
         pltpu.make_async_copy(feat_ref, blocks.at[0], load_sem.at[0]),
         pltpu.make_async_copy(key_ref, keys.at[0], load_sem.at[1]),
+        pltpu.make_async_copy(owner_ref, owner_smem, load_sem.at[2]),
     ]
     for copy in loads:
         copy.start()
-    far = list(range(2, group, 2))
     barrier = pltpu.get_barrier_semaphore()
-    for mask in [1] + far:
+    for mask in range(1, group):
         pl.semaphore_signal(barrier, inc=1, device_id=peer(mask), device_id_type=MESH)
     if n_line <= 8:
         for step in range(1, n_line):
@@ -58,10 +59,13 @@
             return c
         lax.fori_loop(1, n_line, greet, 0)
 
+    for copy in loads:
+        copy.wait()
+
     lane = lax.broadcasted_iota(jnp.int32, (1, LANES), 1)
     inverse = jnp.zeros((1, LANES), jnp.int32)
     for k in range(nkeys):
-        inverse = jnp.where(lane == owner_ref[k], k + 1, inverse)
+        inverse = jnp.where(lane == owner_smem[k], k + 1, inverse)
     row = lax.broadcasted_iota(jnp.int32, (padded + TAIL, 1), 0)
 
     def base_of(step):
@@ -86,16 +90,24 @@
         turned = pltpu.roll(block, (width - offset) % width, 1)
         return jnp.transpose(turned)[:padded]
 
-    def piece(slot, step, first, block, key_row, flat):
+    def halves(value):
+        high = value.astype(jnp.bfloat16)
+        return high, (value - high.astype(jnp.float32)).astype(jnp.bfloat16)
+
+    def with_ones(flat):
+        high, low = halves(jnp.concatenate([flat, jnp.ones((TAIL, nrows), jnp.float32)], axis=0))
+        return jnp.concatenate([high, low], axis=1)
+
+    def piece(step, first, block, right, key_row, left):
         want = wants[step] if unroll else wanted(step)
-        if flat is None:
-            flat = values(block, step)
-        flat = jnp.concatenate([flat, jnp.ones((TAIL, nrows), jnp.float32)], axis=0)
-        picked = jnp.where(key_row == want, flat, 0.0)
-        gram = jnp.dot(
-            picked, block, precision=lax.Precision.HIGHEST, preferred_element_type=jnp.float32
-        )
-        count = jnp.sum(picked[padded:], axis=1, keepdims=True)
+        if left is None:
+            left = with_ones(values(block, step))
+        mask = jnp.where(key_row == want, 1.0, 0.0)
+        mask16 = mask.astype(jnp.bfloat16)
+        picked = left * jnp.concatenate([mask16, mask16], axis=1)
+        gram = jnp.dot(picked, right, preferred_element_type=jnp.float32)
+        gram = gram[:, :width] + gram[:, width:]
+        count = jnp.sum(mask[padded:], axis=1, keepdims=True)
         tail_row = lax.broadcasted_iota(jnp.int32, (TAIL, width), 0)
         tail = jnp.where(tail_row < TAIL // 2, gram[padded:], count)
         if first:
@@ -117,15 +129,17 @@
         key_row = jnp.concatenate(
             [keys[slot, i : i + 1, :] for i in range(nrows // LANES)], axis=1
         )
-        flat = values(block, 0) if shared else None
+        right = jnp.concatenate(halves(block), axis=1)
+        right = jnp.concatenate([right, right], axis=0)
+        left = with_ones(values(block, 0)) if shared else None
         if unroll:
             for step in list(range(1, n_line)) + [0]:
-                piece(slot, step, first, block, key_row, flat)
+                piece(step, first, block, right, key_row, left)
                 if final and step:
                     line_copy(step).start()
         else:
             def body(step, c):
-                piece(slot, step, first, block, key_row, flat)
+                piece(step, first, block, right, key_row, left)
                 return c
             lax.fori_loop(0, n_line, body, 0)
             if final:
@@ -134,53 +148,78 @@
                     return c
                 lax.fori_loop(1, n_line, send, 0)
 
-    def copies(src, dst, device, index):
-        return [
-            pltpu.make_async_remote_copy(
-                src_ref=buf.at[src], dst_ref=buf.at[dst],
-                send_sem=send_sem.at[i, index], recv_sem=recv_sem.at[i, dst],
-                device_id=device, device_id_type=MESH,
-            )
-            for i, buf in enumerate((keys, blocks))
-        ]
-
-    for copy in loads:
-        copy.wait()
-    n_meet = len(far) + n_line
-    pl.semaphore_wait(barrier, n_meet)
+    half_rows = nrows // 2
+
+    def half_copy(src, dst, half, device, index):
+        rows = pl.ds(half * half_rows, half_rows)
+        return pltpu.make_async_remote_copy(
+            src_ref=blocks.at[src, rows], dst_ref=blocks.at[dst, rows],
+            send_sem=send_sem.at[index], recv_sem=recv_sem.at[dst, half],
+            device_id=device, device_id_type=MESH,
+        )
+
+    def key_copy(mask):
+        return pltpu.make_async_remote_copy(
+            src_ref=keys.at[0], dst_ref=keys.at[mask],
+            send_sem=key_send.at[mask], recv_sem=key_recv.at[mask],
+            device_id=peer(mask), device_id_type=MESH,
+        )
+
+    pl.semaphore_wait(barrier, group - 1 + n_line - 1)
 
     sent = []
 
-    def send(src, dst, device):
-        for copy in copies(src, dst, device, len(sent)):
-            copy.start()
-        sent.append((src, dst, device, len(sent)))
-
-    def receive(slot):
-        for copy in copies(slot, slot, peer(1), 0):
-            copy.wait_recv()
-
-    for mask in far:
-        send(0, mask, peer(mask))
-    send(0, 1, peer(1))
+    def send(src, dst, half, device):
+        item = (src, dst, half, device, len(sent))
+        half_copy(*item).start()
+        sent.append(item)
+
+    def receive(slot, half):
+        half_copy(slot, slot, half, peer(1), 0).wait_recv()
+
+    def hand_over(slot, half):
+        send(slot, slot ^ 1, half, peer(1))
+
+    def partner_block(slot):
+        receive(slot, 0)
+        receive(slot, 1)
+
+    send(0, 2, 0, peer(2))
+    send(0, 4, 1, peer(4))
+    send(0, 2, 1, peer(2))
+    send(0, 4, 0, peer(4))
+    send(0, 1, 0, peer(1))
+    send(0, 1, 1, peer(1))
+    for mask in range(1, group):
+        key_copy(mask).start()
+    for mask in range(1, group):
+        key_copy(mask).wait_recv()
     compute(0, first=True)
-    receive(1)
+    partner_block(1)
     compute(1)
-    near = far[:-1]
-    for mask in near:
-        receive(mask)
-        send(mask, mask ^ 1, peer(1))
-    for mask in near:
-        compute(mask)
-    for mask in near:
-        receive(mask ^ 1)
-        compute(mask ^ 1)
-    for mask in far[-1:]:
-        receive(mask)
-        send(mask, mask ^ 1, peer(1))
-        compute(mask)
-        receive(mask ^ 1)
-        compute(mask ^ 1, final=True)
+    receive(2, 0)
+    send(2, 6, 0, peer(4))
+    hand_over(2, 0)
+    receive(4, 1)
+    send(4, 6, 1, peer(2))
+    hand_over(4, 1)
+    receive(2, 1)
+    hand_over(2, 1)
+    receive(4, 0)
+    hand_over(4, 0)
+    compute(2)
+    compute(4)
+    partner_block(3)
+    compute(3)
+    partner_block(5)
+    compute(5)
+    receive(6, 0)
+    hand_over(6, 0)
+    receive(6, 1)
+    hand_over(6, 1)
+    compute(6)
+    partner_block(7)
+    compute(7, final=True)
 
     def collect(step, total):
         line_copy(step).wait_recv()
@@ -211,8 +250,9 @@
     out_ref[...] = result[:length]
 
     for item in sent:
-        for copy in copies(*item):
-            copy.wait_send()
+        half_copy(*item).wait_send()
+    for mask in range(1, group):
+        key_copy(mask).wait_send()
     if unroll:
         for step in range(1, n_line):
             line_copy(step).wait_send()
@@ -225,8 +265,9 @@
 
 def solution(mesh):
     n_rows, n_grp = mesh.shape["rows"], mesh.shape["grp"]
-    inner = 2
-    group = inner * n_grp
+    group = 8
+    inner = group // n_grp
+    assert inner * n_grp == group and n_rows % inner == 0
 
     def local(features, key_ids, owner):
         nkeys = owner.shape[0]
@@ -234,26 +275,28 @@
         length = nkeys * width // (n_rows * n_grp)
         padded = -(-length // 8) * 8
         n_line = n_rows // inner
-        assert padded <= width == LANES and nkeys <= LANES and group & (group - 1) == 0
+        assert padded <= width == LANES and nkeys <= LANES and rows % (2 * LANES) == 0
         keys = key_ids.reshape(rows // LANES, LANES)
-        n_sent = group
         return pl.pallas_call(
             functools.partial(kernel, inner, n_grp, n_line, nkeys, length, padded),
             out_shape=jax.ShapeDtypeStruct((length, width), jnp.float32),
             in_specs=[
                 pl.BlockSpec(memory_space=pltpu.MemorySpace.HBM),
                 pl.BlockSpec(memory_space=pltpu.MemorySpace.HBM),
-                pl.BlockSpec(memory_space=pltpu.MemorySpace.SMEM),
+                pl.BlockSpec(memory_space=pltpu.MemorySpace.HBM),
             ],
             out_specs=pl.BlockSpec(memory_space=pltpu.MemorySpace.VMEM),
             scratch_shapes=[
+                pltpu.SMEM((nkeys,), jnp.int32),
                 pltpu.VMEM((group, rows, width), jnp.float32),
                 pltpu.VMEM((group, rows // LANES, LANES), jnp.int32),
                 pltpu.VMEM((n_line, padded + TAIL, width), jnp.float32),
                 pltpu.VMEM((n_line, padded + TAIL, width), jnp.float32),
-                pltpu.SemaphoreType.DMA((2,)),
-                pltpu.SemaphoreType.DMA((2, n_sent)),
-                pltpu.SemaphoreType.DMA((2, group)),
+                pltpu.SemaphoreType.DMA((3,)),
+                pltpu.SemaphoreType.DMA((2 * group - 2,)),
+                pltpu.SemaphoreType.DMA((group, 2)),
+                pltpu.SemaphoreType.DMA((group,)),
+                pltpu.SemaphoreType.DMA((group,)),
                 pltpu.SemaphoreType.DMA((n_line,)),
                 pltpu.SemaphoreType.DMA((n_line,)),
             ],

time: 23.9 us -> 23.8 us (level); the launches traced: 23.7 us -> 23.3 us
  Pallas kernels: 22.2 us -> 21.9 us
    pallas_call x1, Pallas kernels: 22.2 us -> 21.9 us  [local(): pl.pallas_call(functools.partial(kernel, inner, n_grp, n_line, nkeys, len...]
where the time goes in v2:
time: 23.8 us; the launch traced here: 23.3 us
  Pallas kernels  21.9 us (92%)
  local copies, waits for them, and re-layouts  1.42 us (6%)
    pallas_call x1, Pallas kernels, local(): pl.pallas_call(functools.partial(kernel, inner, n_grp, n_line, nkeys, len...  21.9 us
    unnamed x1, local copies, waits for them, and re-layouts  1.42 us

profile of v2, /device:TPU:0, one launch (start us, length us, event | category | flops | bytes accessed | tf_op | source)
XLA Modules:
  0.0 23.3 jit_solution(13776020651336033995)
XLA Ops:
  0.0 21.9 %shard_map.37 = f32[96,128]{1,0:T(8,128)} custom-call(f32[256,128]{1,0:T(8,128)} %feat_ref.1, s32[2,128]{1,0:T(2,128)} %bitcast.1, s32[24]{0:T(128)} %owner_ref.1), custom_call_target="tpu_custom_call" | custom-call | tf_op jit(solution)/shard_map/pallas_call | solution.py:280
  21.9 1.4 %copy.5 = f32[96,128]{1,0:T(8,128)} copy(f32[96,128]{1,0:T(8,128)} %shard_map.37) | data formatting | bytes 98304

commit v3 on v2

--- a/solution.py
+++ b/solution.py
@@ -48,7 +48,7 @@
     for copy in loads:
         copy.start()
     barrier = pltpu.get_barrier_semaphore()
-    for mask in range(1, group):
+    for mask in (1, 2, 4):
         pl.semaphore_signal(barrier, inc=1, device_id=peer(mask), device_id_type=MESH)
     if n_line <= 8:
         for step in range(1, n_line):
@@ -150,6 +150,13 @@
 
     half_rows = nrows // 2
 
+    def key_copy(src, dst, device):
+        return pltpu.make_async_remote_copy(
+            src_ref=keys.at[src], dst_ref=keys.at[dst],
+            send_sem=key_send.at[dst], recv_sem=key_recv.at[dst],
+            device_id=device, device_id_type=MESH,
+        )
+
     def half_copy(src, dst, half, device, index):
         rows = pl.ds(half * half_rows, half_rows)
         return pltpu.make_async_remote_copy(
@@ -158,23 +165,20 @@
             device_id=device, device_id_type=MESH,
         )
 
-    def key_copy(mask):
-        return pltpu.make_async_remote_copy(
-            src_ref=keys.at[0], dst_ref=keys.at[mask],
-            send_sem=key_send.at[mask], recv_sem=key_recv.at[mask],
-            device_id=peer(mask), device_id_type=MESH,
-        )
-
-    pl.semaphore_wait(barrier, group - 1 + n_line - 1)
+    pl.semaphore_wait(barrier, 3 + n_line - 1)
 
     sent = []
 
     def send(src, dst, half, device):
         item = (src, dst, half, device, len(sent))
+        if half == 0:
+            key_copy(src, dst, device).start()
         half_copy(*item).start()
         sent.append(item)
 
     def receive(slot, half):
+        if half == 0:
+            key_copy(slot, slot, peer(1)).wait_recv()
         half_copy(slot, slot, half, peer(1), 0).wait_recv()
 
     def hand_over(slot, half):
@@ -190,10 +194,6 @@
     send(0, 4, 0, peer(4))
     send(0, 1, 0, peer(1))
     send(0, 1, 1, peer(1))
-    for mask in range(1, group):
-        key_copy(mask).start()
-    for mask in range(1, group):
-        key_copy(mask).wait_recv()
     compute(0, first=True)
     partner_block(1)
     compute(1)
@@ -251,8 +251,9 @@
 
     for item in sent:
         half_copy(*item).wait_send()
-    for mask in range(1, group):
-        key_copy(mask).wait_send()
+    for item in sent:
+        if item[2] == 0:
+            key_copy(item[0], item[1], item[3]).wait_send()
     if unroll:
         for step in range(1, n_line):
             line_copy(step).wait_send()

time: 23.8 us -> 21.9 us (0.920); the launches traced: 23.3 us -> 21.8 us
  Pallas kernels: 21.9 us -> 20.3 us
    pallas_call x1, Pallas kernels: 21.9 us -> 20.3 us  [local(): pl.pallas_call(functools.partial(kernel, inner, n_grp, n_line, nkeys, len...]
where the time goes in v3:
time: 21.9 us; the launch traced here: 21.8 us
  Pallas kernels  20.3 us (93%)
  local copies, waits for them, and re-layouts  1.42 us (6%)
    pallas_call x1, Pallas kernels, local(): pl.pallas_call(functools.partial(kernel, inner, n_grp, n_line, nkeys, len...  20.3 us
    unnamed x1, local copies, waits for them, and re-layouts  1.42 us

profile of v3, /device:TPU:0, one launch (start us, length us, event | category | flops | bytes accessed | tf_op | source)
XLA Modules:
  0.0 21.8 jit_solution(16994643790354013828)
XLA Ops:
  0.0 20.3 %shard_map.37 = f32[96,128]{1,0:T(8,128)} custom-call(f32[256,128]{1,0:T(8,128)} %feat_ref.1, s32[2,128]{1,0:T(2,128)} %bitcast.1, s32[24]{0:T(128)} %owner_ref.1), custom_call_target="tpu_custom_call" | custom-call | tf_op jit(solution)/shard_map/pallas_call | solution.py:281
  20.3 1.4 %copy.5 = f32[96,128]{1,0:T(8,128)} copy(f32[96,128]{1,0:T(8,128)} %shard_map.37) | data formatting | bytes 98304
